TPU v7x, 32 devices: a whole 2x2x4 slice. The times are simulated.
32 devices in a mesh: dp: 16 (over z, y, core), tensor: 2 (over x).
Axes of the slice: x: 2, y: 2, z: 4, core: 2. Of those that a mesh axis runs over, the one named last changes fastest.
Arguments:
- expert_act: bfloat16 [16384, 2880], P(('dp', 'tensor')), may hold values from -6 to 6
- grad_out: bfloat16 [32768, 1440], P(('dp', 'tensor')), may hold values from -6 to 6
- slot_token: int32 [16384], P(('dp', 'tensor')), may hold values from 0 to 1023, as said below
- slot_prob: float32 [16384], P(('dp', 'tensor')), may hold values from 0.2 to 1
- live_count: int32 [32], P(('dp', 'tensor')), may hold values from 128 to 512, as said below
Outputs:
- weight_grad: float32 [2880, 1440], P('dp', 'tensor')
Inputs may be any that keep to these rules, and one draw needn't show every extreme that they name: `slot_token`: each device's 512 entries are distinct token indices of that device. `live_count`: each entry is 512 // j for some j of 1 to 4.
All inputs are finite; a program needn't handle non-finite values.
Results may differ from a plain program's by a relative error of at most 0.0029.
Values may be sent and summed in bfloat16 or wider, within the bound.
A program may use at most 128 MiB of HBM per device.

v0:
```python
import math

import jax
import jax.numpy as jnp
from jax import lax
from jax.sharding import PartitionSpec as P


def contract(left, right):
    return lax.dot_general(
        left, right, (((0,), (0,)), ((), ())), preferred_element_type=jnp.float32
    )


def shards(expert_act, grad_out, slot_token, slot_prob, live_count):
    slot_count = expert_act.shape[0]
    devices = lax.axis_size("dp") * lax.axis_size("tensor")
    scaling = 1.0 / math.sqrt(slot_count * devices)
    position = jnp.arange(slot_count, dtype=jnp.int32)
    live_mask = position < live_count[0]
    weighting = jnp.where(live_mask, slot_prob, jnp.zeros_like(slot_prob))
    picked = jnp.take(grad_out, slot_token, axis=0).astype(jnp.float32)
    weighted = (picked * weighting[:, None]).astype(jnp.bfloat16)
    both_acts = lax.all_gather(expert_act, "tensor", axis=0, tiled=True)
    both_grads = lax.all_to_all(weighted, "tensor", split_axis=1, concat_axis=0, tiled=True)
    gradient = lax.psum_scatter(
        contract(both_acts, both_grads), "dp", scatter_dimension=0, tiled=True
    )
    return gradient * scaling


def solution(mesh):
    return jax.shard_map(
        shards,
        mesh=mesh,
        in_specs=(
            P(("dp", "tensor"), None),
            P(("dp", "tensor"), None),
            P(("dp", "tensor")),
            P(("dp", "tensor")),
            P(("dp", "tensor")),
        ),
        out_specs=P("dp", "tensor"),
        check_vma=False,
    )
```

profile of v0, /device:TPU:0, one launch (start us, length us, event | category | flops | bytes accessed | tf_op | source)
XLA Modules:
  0.0 293.3 jit_solution(11381292390871192183)
XLA Ops:
  6.5 0.0 all-gather.2.cloned.1.call-start
  6.5 0.7 all-gather.2.cloned.1.call-update
  7.3 0.0 copy-start
  7.3 0.0 all-reduce.3.cloned.1.call-start
  7.3 3.1 %copy.16 = bf16[1024,1440]{1,0:T(8,128)(2,1)S(1)} copy(bf16[1024,1440]{0,1:T(8,128)(2,1)} %param.6) | data formatting | bytes 5898240 | tf_op args[1]
  10.5 0.0 copy-done
  10.5 3.0 %gather_fusion = bf16[512,1440]{1,0:T(8,128)(2,1)} fusion(bf16[1024,1440]{1,0:T(8,128)(2,1)S(1)} %copy.16, s32[1024]{0:T(1024)S(1)} %pad_clamp_fusion), kind=kCustom, calls=%fused_computation | custom fusion | bytes 2951168 | tf_op jit(solution)/shard_map/jit(_take)/gather | solution.py:22
  13.5 0.0 copy-start.1
  13.5 1.7 copy.17
  15.8 0.0 copy-done.1
  15.9 0.4 multiply_convert_fusion
  16.3 37.9 %all_to_all.16 = bf16[512,2,720]{0,2,1:T(8,128)(2,1)S(1)} all-to-all(bf16[512,2,720]{0,2,1:T(8,128)(2,1)S(1)} %multiply_convert_fusion), channel_id=1, replica_groups=mesh['dp'=16,'tensor'=2] {'tensor'}, dimensions={1} | all-to-all | bytes 2949120 | tf_op jit(solution)/shard_map/all_to_all | solution.py:25
  54.1 0.2 copy.22
  54.3 47.6 %all-gather.2.cloned.1.call-done = bf16[1024,2880]{0,1:T(8,128)(2,1)} async-done(((bf16[512,2880]{0,1:T(8,128)(2,1)}), bf16[1024,2880]{0,1:T(8,128)(2,1)}) %all-gather.2.cloned.1.call-update) | async-done | bytes 5898256 | tf_op jit(solution)/shard_map/all_gather | solution.py:24
  101.9 9.6 %convolution_bitcast_fusion = f32[2880,720]{0,1:T(8,128)} fusion(bf16[1024,720]{0,1:T(8,128)(2,1)S(1)} %bitcast.15, bf16[1024,2880]{0,1:T(8,128)(2,1)} %all-gather.2.cloned.1.call-done), kind=kOutput, calls=%fused_computation.1 | convolution fusion | flops 4246732800 | bytes 15667200 | tf_op jit(solution)/shard_map/dot_general | solution.py:10
  111.5 0.0 copy-start.2
  111.5 0.0 all-reduce.3.cloned.1.call-update
  111.6 0.6 copy-done.2
  112.2 0.6 dynamic-slice
  113.4 170.4 %all-reduce.3.cloned.1.call-done = f32[2880,720]{0,1:T(8,128)} async-done(((f32[2880,720]{0,1:T(8,128)}), f32[2880,720]{0,1:T(8,128)}) %all-reduce.3.cloned.1.call-update) | async-done | bytes 8294416
  283.8 1.5 constant_dynamic-slice_fusion
  285.3 0.2 copy.19
  285.6 0.8 broadcast_multiply_fusion
  (4 shorter events, 0.0 us)
Async XLA Ops:
  6.5 95.4 %all-gather.2.cloned.1.call-start = ((), (), s32[]{:S(2)}) async-start(), calls=%async_computation.1 | async-start | bytes 8847360 | tf_op jit(solution)/shard_map/all_gather | solution.py:24
  7.3 3.2 %copy-start = (s32[512]{0:T(512)S(1)}, s32[512]{0:T(512)}, u32[]{:S(2)}) copy-start(s32[512]{0:T(512)} %param.7) | copy-start | bytes 6148
  7.3 276.6 %all-reduce.3.cloned.1.call-start = ((), (), s32[]{:S(2)}) async-start(), calls=%async_computation.2 | async-start | bytes 16957440
  13.5 2.4 copy-start.1
  111.5 0.7 copy-start.2
Sparse Core Ops, SparseCore 0:
  8.9 92.9 all-gather.1
  111.7 172.0 all-reduce.2
where the time goes:
time: 294 us; the launch traced here: 293 us
  waiting for transfers between devices  219 us (74%)
  blocking collectives  37.9 us (13%)
  between operations  14.8 us (5%)
  local copies, waits for them, and re-layouts  10.9 us (4%)
  matrix products  9.64 us (3%)
    unnamed x3, waiting for transfers between devices  171 us
    all_gather x1, waiting for transfers between devices, shards(): both_acts = lax.all_gather(expert_act, 'tensor', axis=0, tiled=True)  47.6 us
    all_to_all x1, blocking collectives, shards(): lax.all_to_all(weighted, 'tensor', split_axis=1, concat_axis=0, tiled=True)  37.9 us
    dot_general x1, matrix products, contract(): lax.dot_general(left, right, (((0,), (0,)), ((), ())), preferred_element_...  9.64 us
  transfers between devices with their start and end apart: 2, of which 2 were waited for; matrix products, arithmetic and copies ran while one was open for 3% of the time, Pallas kernels for 0%

commit v1 on v0

v1 whole, which is shorter than its diff:
```python
import functools
import math

import jax
import jax.numpy as jnp
from jax import lax
from jax.experimental import pallas as pl
from jax.experimental.pallas import tpu as pltpu
from jax.sharding import PartitionSpec as P

MESH = pl.DeviceIdType.MESH


def kernel(
    outer,
    acts_ref, grad_ref, token_ref, weight_ref, out_ref,
    peer_acts, mine, peer,
    send_a, recv_a, send_b, recv_b, send_z, recv_z,
    pair_sems, a_sems, b_sems, z_sems,
):
    dp = lax.axis_index("dp")
    half = lax.axis_index("tensor")
    core = lax.rem(dp, 2)
    mid = lax.rem(dp // 2, 2)
    own = dp // 4
    my_a = half * (1 - core) + mid * core
    my_b = mid * (1 - core) + half * core
    flip_mid = dp + 2 - 4 * mid
    pair_dev = {"dp": dp + 1 - 2 * core, "tensor": half}
    a_dev = {
        "dp": dp * (1 - core) + flip_mid * core,
        "tensor": (1 - half) * (1 - core) + half * core,
    }
    b_dev = {
        "dp": flip_mid * (1 - core) + dp * core,
        "tensor": half * (1 - core) + (1 - half) * core,
    }

    def z_dev(step):
        return {"dp": dp + (target(step) - own) * 4, "tensor": half}

    def target(step):
        return lax.rem(own + 1 + step, outer)

    def remote(src, dst, sems, device):
        return pltpu.make_async_remote_copy(
            src_ref=src, dst_ref=dst, send_sem=sems[0], recv_sem=sems[1],
            device_id=device, device_id_type=MESH,
        )

    barrier = pltpu.get_barrier_semaphore()
    for device in [pair_dev, a_dev, b_dev] + [z_dev(s) for s in range(outer - 1)]:
        pl.semaphore_signal(barrier, inc=1, device_id=device, device_id_type=MESH)
    pl.semaphore_wait(barrier, outer + 2)

    acts_copy = remote(
        acts_ref.at[1 - core], peer_acts, (pair_sems.at[0], pair_sems.at[1]), pair_dev
    )
    acts_copy.start()

    slots, tokens = token_ref.shape[0], grad_ref.shape[0]
    width = mine.shape[2]
    chosen = lax.broadcasted_iota(jnp.int32, (slots, tokens), 1) == token_ref[...]
    onehot = jnp.where(chosen, 1.0, 0.0).astype(jnp.bfloat16)
    picked = jnp.dot(onehot, grad_ref[...], preferred_element_type=jnp.float32)
    weighted = (picked * weight_ref[...]).astype(jnp.bfloat16)
    mine[0] = weighted[:, :width]
    mine[1] = weighted[:, width:]
    grad_copy = remote(mine, peer, (pair_sems.at[2], pair_sems.at[3]), pair_dev)
    grad_copy.start()
    acts_copy.wait_recv()
    grad_copy.wait_recv()

    def term(step, a, b):
        row = target(step) * 2 + b * (1 - core) + a * core
        column = a * (1 - core) + b * core
        return jnp.dot(
            acts_ref[core, row], mine[column], preferred_element_type=jnp.float32
        ) + jnp.dot(
            peer_acts[row], peer[column], preferred_element_type=jnp.float32
        )

    def copy_a(step, k):
        return remote(
            send_a.at[step, k], recv_a.at[step, k],
            (a_sems.at[0, step, k], a_sems.at[1, step, k]), a_dev,
        )

    def copy_b(step):
        return remote(
            send_b.at[step], recv_b.at[step],
            (b_sems.at[0, step], b_sems.at[1, step]), b_dev,
        )

    def copy_z(step):
        return remote(
            send_z.at[step], recv_z.at[step],
            (z_sems.at[0, step], z_sems.at[1, step]), z_dev(step),
        )

    def first(step, carry):
        for k in range(2):
            b = 1 - my_b if k == 0 else my_b
            send_a[step, k] = term(step, 1 - my_a, b).astype(jnp.bfloat16)
            copy_a(step, k).start()
        return carry

    def second(step):
        total = term(step, my_a, 1 - my_b)
        copy_a(step, 0).wait_recv()
        total = total + recv_a[step, 0].astype(jnp.float32)
        send_b[step] = total.astype(jnp.bfloat16)
        copy_b(step).start()

    def third(step):
        total = term(step, my_a, my_b)
        copy_a(step, 1).wait_recv()
        total = total + recv_a[step, 1].astype(jnp.float32)
        copy_b(step).wait_recv()
        return total + recv_b[step].astype(jnp.float32)

    def later(step, carry):
        second(step)
        send_z[step - 1] = third(step - 1).astype(jnp.bfloat16)
        copy_z(step - 1).start()
        return carry

    lax.fori_loop(0, outer, first, 0)
    second(0)
    lax.fori_loop(1, outer, later, 0)
    out_ref[...] = third(outer - 1)

    def add(step, carry):
        copy_z(step).wait_recv()
        out_ref[...] += recv_z[step].astype(jnp.float32)
        return carry

    lax.fori_loop(0, outer - 1, add, 0)

    def drain(step, carry):
        copy_a(step, 0).wait_send()
        copy_a(step, 1).wait_send()
        copy_b(step).wait_send()
        return carry

    lax.fori_loop(0, outer, drain, 0)

    def drain_z(step, carry):
        copy_z(step).wait_send()
        return carry

    lax.fori_loop(0, outer - 1, drain_z, 0)
    acts_copy.wait_send()
    grad_copy.wait_send()


def shards(expert_act, grad_out, slot_token, slot_prob, live_count):
    slots, hidden = expert_act.shape
    ranks, halves = lax.axis_size("dp"), lax.axis_size("tensor")
    outer = ranks // 4
    rows, columns = hidden // ranks, grad_out.shape[1] // halves
    scaling = 1.0 / math.sqrt(slots * ranks * halves)
    live = jnp.arange(slots, dtype=jnp.int32) < live_count[0]
    weighting = jnp.where(live, slot_prob, jnp.zeros_like(slot_prob))
    acts = expert_act.T.reshape(outer * 2, 2, rows, slots).transpose(1, 0, 2, 3)
    bf16, dma = jnp.bfloat16, pltpu.SemaphoreType.DMA
    total = pl.pallas_call(
        functools.partial(kernel, outer),
        out_shape=jax.ShapeDtypeStruct((rows, columns), jnp.float32),
        in_specs=[pl.BlockSpec(memory_space=pltpu.VMEM)] * 4,
        out_specs=pl.BlockSpec(memory_space=pltpu.VMEM),
        scratch_shapes=[
            pltpu.VMEM((outer * 2, rows, slots), bf16),
            pltpu.VMEM((2, slots, columns), bf16),
            pltpu.VMEM((2, slots, columns), bf16),
            pltpu.VMEM((outer, 2, rows, columns), bf16),
            pltpu.VMEM((outer, 2, rows, columns), bf16),
            pltpu.VMEM((outer, rows, columns), bf16),
            pltpu.VMEM((outer, rows, columns), bf16),
            pltpu.VMEM((outer - 1, rows, columns), bf16),
            pltpu.VMEM((outer - 1, rows, columns), bf16),
            dma((4,)),
            dma((2, outer, 2)),
            dma((2, outer)),
            dma((2, outer - 1)),
        ],
        compiler_params=pltpu.CompilerParams(
            collective_id=0, has_side_effects=True, vmem_limit_bytes=60 * 2**20
        ),
    )(acts, grad_out, slot_token[:, None], weighting[:, None])
    return total * scaling


def solution(mesh):
    return jax.shard_map(
        shards,
        mesh=mesh,
        in_specs=(
            P(("dp", "tensor"), None),
            P(("dp", "tensor"), None),
            P(("dp", "tensor")),
            P(("dp", "tensor")),
            P(("dp", "tensor")),
        ),
        out_specs=P("dp", "tensor"),
        check_vma=False,
    )
```

time: 294 us -> 74.7 us (0.25)
  waiting for transfers between devices: 219 us -> 0 us
  Pallas kernels: 0 us -> 59.4 us
  blocking collectives: 37.9 us -> 0 us
  between operations: 14.8 us -> 0.67 us
  matrix products: 9.64 us -> 0 us
    unnamed x3 -> x0, waiting for transfers between devices: 171 us -> none
    pallas_call x0 -> x1, Pallas kernels: none -> 59.4 us  [shards(): pl.pallas_call(functools.partial(kernel, outer), out_shape=jax.ShapeDtype...]
    all_gather x1 -> x0, waiting for transfers between devices: 47.6 us -> none  [shards(): both_acts = lax.all_gather(expert_act, 'tensor', axis=0, tiled=True)]
    all_to_all x1 -> x0, blocking collectives: 37.9 us -> none  [shards(): lax.all_to_all(weighted, 'tensor', split_axis=1, concat_axis=0, tiled=True)]
    dot_general x1 -> x0, matrix products: 9.64 us -> none  [contract(): lax.dot_general(left, right, (((0,), (0,)), ((), ())), preferred_element_...]
    reshape x0 -> x2, local copies, waits for them, and re-layouts: none -> 4.7 us  [shards(): acts = expert_act.T.reshape(outer * 2, 2, rows, slots).transpose(1, 0, 2, 3)]
    gather x2 -> x0, local copies, waits for them, and re-layouts: 4.67 us -> none  [shards(): picked = jnp.take(grad_out, slot_token, axis=0).astype(jnp.float32)]
  transfers between devices with their start and end apart: 2 -> 0, of which waited for: 2 -> 0; matrix products, arithmetic and copies ran while one was open for 3% -> 0% of each run, Pallas kernels for 0% -> 0%
where the time goes in v1:
time: 74.7 us; the launch traced here: 74.3 us
  Pallas kernels  59.4 us (80%)
  local copies, waits for them, and re-layouts  11.7 us (16%)
  other arithmetic  2.59 us (3%)
    pallas_call x1, Pallas kernels, shards(): pl.pallas_call(functools.partial(kernel, outer), out_shape=jax.ShapeDtype...  59.4 us
    reshape x2, local copies, waits for them, and re-layouts, shards(): acts = expert_act.T.reshape(outer * 2, 2, rows, slots).transpose(1, 0, 2, 3)  4.7 us
    unnamed x1, local copies, waits for them, and re-layouts  4.61 us
    mul x1, other arithmetic, shards(): return total * scaling  1.9 us
    broadcast_in_dim x1, local copies, waits for them, and re-layouts, shards(): slot_token[:, None]  1.53 us

profile of v1, /device:TPU:0, one launch (start us, length us, event | category | flops | bytes accessed | tf_op | source)
XLA Modules:
  0.0 74.3 jit_solution(3137504280011026743)
XLA Ops:
  0.7 0.7 fusion
  1.3 0.9 %copy.10.weight_ref = f32[512,1]{1,0:T(8,128)} copy(f32[512,1]{0,1:T(1,128)S(1)} %bitcast.10) | data formatting | bytes 4096 | tf_op jit(solution)/shard_map/broadcast_in_dim | solution.py:190
  2.2 1.5 %copy.9.token_ref = s32[512,1]{1,0:T(8,128)} copy(s32[512,1]{0,1:T(1,128)} %bitcast.11) | data formatting | bytes 4096 | tf_op jit(solution)/shard_map/broadcast_in_dim | solution.py:190
  3.7 2.8 %reshape.3 = bf16[8,2,180,512]{3,2,1,0:T(8,128)(2,1)S(1)} reshape(bf16[2880,512]{1,0:T(8,128)(2,1)} %bitcast.9) | data formatting | bytes 5898240 | tf_op jit(solution)/shard_map/reshape | solution.py:165
  6.5 1.9 %copy.12 = bf16[8,2,180,512]{3,2,0,1:T(8,128)(2,1)} copy(bf16[8,2,180,512]{3,2,1,0:T(8,128)(2,1)S(1)} %reshape.3) | data formatting | bytes 5898240 | tf_op jit(solution)/shard_map/reshape | solution.py:165
  8.5 4.6 %copy.8.grad_ref = bf16[1024,1440]{1,0:T(8,128)(2,1)} copy(bf16[1024,1440]{0,1:T(8,128)(2,1)} %param.6) | data formatting | bytes 5898240 | tf_op args[1]
  13.1 59.4 %shard_map.55 = f32[180,720]{1,0:T(8,128)} custom-call(bf16[2,8,180,512]{3,2,1,0:T(8,128)(2,1)} %bitcast.8, bf16[1024,1440]{1,0:T(8,128)(2,1)} %copy.8.grad_ref, s32[512,1]{1,0:T(8,128)} %copy.9.token_ref, f32[512,1]{1,0:T(8,128)} %copy.10.weight_ref), custom_call_target="tpu_custom_call" | custom-call | tf_op jit(solution)/shard_map/pallas_call | solution.py:167
  72.4 1.9 %broadcast_multiply_fusion = f32[180,720]{1,0:T(8,128)} fusion(f32[180,720]{1,0:T(8,128)} %shard_map.55), kind=kLoop, calls=%fused_computation.1 | loop fusion | flops 129600 | bytes 1036800 | tf_op jit(solution)/shard_map/mul | solution.py:191

commit v2 on v1

--- a/solution.py
+++ b/solution.py
@@ -13,10 +13,10 @@
 
 def kernel(
     outer,
-    acts_ref, grad_ref, token_ref, weight_ref, out_ref,
-    peer_acts, mine, peer,
+    acts_hbm, grad_hbm, token_ref, prob_ref, live_ref, out_ref,
+    acts_raw, grad_raw, acts, peer_acts, mine, peer,
     send_a, recv_a, send_b, recv_b, send_z, recv_z,
-    pair_sems, a_sems, b_sems, z_sems,
+    load_sems, pair_sems, a_sems, b_sems, z_sems,
 ):
     dp = lax.axis_index("dp")
     half = lax.axis_index("tensor")
@@ -48,36 +48,61 @@
             device_id=device, device_id_type=MESH,
         )
 
+    load_acts = pltpu.make_async_copy(acts_hbm, acts_raw, load_sems.at[0])
+    load_acts.start()
+    grad_order = (1 - half, half)
+    load_grads = [
+        pltpu.make_async_copy(grad_hbm.at[g], grad_raw.at[g], load_sems.at[1 + i])
+        for i, g in enumerate(grad_order)
+    ]
+    for load in load_grads:
+        load.start()
+
     barrier = pltpu.get_barrier_semaphore()
     for device in [pair_dev, a_dev, b_dev] + [z_dev(s) for s in range(outer - 1)]:
         pl.semaphore_signal(barrier, inc=1, device_id=device, device_id_type=MESH)
+
+    slots, tokens = token_ref.shape[1], grad_raw.shape[2]
+    chosen = lax.broadcasted_iota(jnp.int32, (tokens, slots), 0) == token_ref[...]
+    onehot = jnp.where(chosen, 1.0, 0.0).astype(jnp.bfloat16)
+    live = lax.broadcasted_iota(jnp.int32, (1, slots), 1) < live_ref[0]
+    weight = jnp.where(live, prob_ref[...], 0.0)
+
+    load_acts.wait()
+    rows = acts.shape[2]
+    for k in range(outer * 4):
+        acts[k % 2, k // 2] = acts_raw[k * rows : (k + 1) * rows, :]
     pl.semaphore_wait(barrier, outer + 2)
-
     acts_copy = remote(
-        acts_ref.at[1 - core], peer_acts, (pair_sems.at[0], pair_sems.at[1]), pair_dev
+        acts.at[1 - core], peer_acts, (pair_sems.at[0], pair_sems.at[1]), pair_dev
     )
     acts_copy.start()
 
-    slots, tokens = token_ref.shape[0], grad_ref.shape[0]
-    width = mine.shape[2]
-    chosen = lax.broadcasted_iota(jnp.int32, (slots, tokens), 1) == token_ref[...]
-    onehot = jnp.where(chosen, 1.0, 0.0).astype(jnp.bfloat16)
-    picked = jnp.dot(onehot, grad_ref[...], preferred_element_type=jnp.float32)
-    weighted = (picked * weight_ref[...]).astype(jnp.bfloat16)
-    mine[0] = weighted[:, :width]
-    mine[1] = weighted[:, width:]
-    grad_copy = remote(mine, peer, (pair_sems.at[2], pair_sems.at[3]), pair_dev)
-    grad_copy.start()
+    grad_copies = []
+    for i, g in enumerate(grad_order):
+        load_grads[i].wait()
+        picked = jnp.dot(grad_raw[g], onehot, preferred_element_type=jnp.float32)
+        mine[g] = (picked * weight).astype(jnp.bfloat16)
+        copy = remote(
+            mine.at[g], peer.at[g],
+            (pair_sems.at[2 + 2 * i], pair_sems.at[3 + 2 * i]), pair_dev,
+        )
+        copy.start()
+        grad_copies.append(copy)
     acts_copy.wait_recv()
-    grad_copy.wait_recv()
+    for copy in grad_copies:
+        copy.wait_recv()
+
+    def contract(left, right):
+        return lax.dot_general(
+            left, right, (((1,), (1,)), ((), ())), preferred_element_type=jnp.float32
+        )
 
     def term(step, a, b):
         row = target(step) * 2 + b * (1 - core) + a * core
         column = a * (1 - core) + b * core
-        return jnp.dot(
-            acts_ref[core, row], mine[column], preferred_element_type=jnp.float32
-        ) + jnp.dot(
-            peer_acts[row], peer[column], preferred_element_type=jnp.float32
+        return contract(acts[core, row], mine[column]) + contract(
+            peer_acts[row], peer[column]
         )
 
     def copy_a(step, k):
@@ -151,35 +176,44 @@
 
     lax.fori_loop(0, outer - 1, drain_z, 0)
     acts_copy.wait_send()
-    grad_copy.wait_send()
+    for copy in grad_copies:
+        copy.wait_send()
 
 
 def shards(expert_act, grad_out, slot_token, slot_prob, live_count):
     slots, hidden = expert_act.shape
+    tokens = grad_out.shape[0]
     ranks, halves = lax.axis_size("dp"), lax.axis_size("tensor")
     outer = ranks // 4
     rows, columns = hidden // ranks, grad_out.shape[1] // halves
     scaling = 1.0 / math.sqrt(slots * ranks * halves)
-    live = jnp.arange(slots, dtype=jnp.int32) < live_count[0]
-    weighting = jnp.where(live, slot_prob, jnp.zeros_like(slot_prob))
-    acts = expert_act.T.reshape(outer * 2, 2, rows, slots).transpose(1, 0, 2, 3)
     bf16, dma = jnp.bfloat16, pltpu.SemaphoreType.DMA
     total = pl.pallas_call(
         functools.partial(kernel, outer),
         out_shape=jax.ShapeDtypeStruct((rows, columns), jnp.float32),
-        in_specs=[pl.BlockSpec(memory_space=pltpu.VMEM)] * 4,
+        in_specs=[
+            pl.BlockSpec(memory_space=pl.ANY),
+            pl.BlockSpec(memory_space=pl.ANY),
+            pl.BlockSpec(memory_space=pltpu.VMEM),
+            pl.BlockSpec(memory_space=pltpu.VMEM),
+            pl.BlockSpec(memory_space=pltpu.SMEM),
+        ],
         out_specs=pl.BlockSpec(memory_space=pltpu.VMEM),
         scratch_shapes=[
+            pltpu.VMEM((hidden, slots), bf16),
+            pltpu.VMEM((halves, columns, tokens), bf16),
+            pltpu.VMEM((2, outer * 2, rows, slots), bf16),
             pltpu.VMEM((outer * 2, rows, slots), bf16),
-            pltpu.VMEM((2, slots, columns), bf16),
-            pltpu.VMEM((2, slots, columns), bf16),
+            pltpu.VMEM((halves, columns, slots), bf16),
+            pltpu.VMEM((halves, columns, slots), bf16),
             pltpu.VMEM((outer, 2, rows, columns), bf16),
             pltpu.VMEM((outer, 2, rows, columns), bf16),
             pltpu.VMEM((outer, rows, columns), bf16),
             pltpu.VMEM((outer, rows, columns), bf16),
             pltpu.VMEM((outer - 1, rows, columns), bf16),
             pltpu.VMEM((outer - 1, rows, columns), bf16),
-            dma((4,)),
+            dma((3,)),
+            dma((6,)),
             dma((2, outer, 2)),
             dma((2, outer)),
             dma((2, outer - 1)),
@@ -187,7 +221,13 @@
         compiler_params=pltpu.CompilerParams(
             collective_id=0, has_side_effects=True, vmem_limit_bytes=60 * 2**20
         ),
-    )(acts, grad_out, slot_token[:, None], weighting[:, None])
+    )(
+        expert_act.T,
+        grad_out.T.reshape(halves, columns, tokens),
+        slot_token[None, :],
+        slot_prob[None, :],
+        live_count,
+    )
     return total * scaling
 
 

time: 74.7 us -> 60.6 us (0.81)
  local copies, waits for them, and re-layouts: 11.7 us -> 0 us
  Pallas kernels: 59.4 us -> 57.9 us
    reshape x2 -> x0, local copies, waits for them, and re-layouts: 4.7 us -> none  [shards(): acts = expert_act.T.reshape(outer * 2, 2, rows, slots).transpose(1, 0, 2, 3)]
    unnamed x1 -> x0, local copies, waits for them, and re-layouts: 4.61 us -> none
    broadcast_in_dim x2 -> x0, local copies, waits for them, and re-layouts: 2.4 us -> none  [the longest x1 1.53 us: shards(): slot_token[:, None]]
    pallas_call x1, Pallas kernels: 59.4 us -> 57.9 us  [shards(): pl.pallas_call(functools.partial(kernel, outer), out_shape=jax.ShapeDtype...]
where the time goes in v2:
time: 60.6 us; the launch traced here: 60.4 us
  Pallas kernels  57.9 us (96%)
  other arithmetic  1.9 us (3%)
  between operations  0.66 us (1%)
    pallas_call x1, Pallas kernels, shards(): pl.pallas_call(functools.partial(kernel, outer), out_shape=jax.ShapeDtype...  57.9 us
    mul x1, other arithmetic, shards(): return total * scaling  1.9 us

profile of v2, /device:TPU:0, one launch (start us, length us, event | category | flops | bytes accessed | tf_op | source)
XLA Modules:
  0.0 60.4 jit_solution(14020441362489567351)
XLA Ops:
  0.7 57.9 %shard_map.55 = f32[180,720]{1,0:T(8,128)} custom-call(bf16[2880,512]{1,0:T(8,128)(2,1)} %bitcast.6, bf16[2,720,1024]{2,1,0:T(8,128)(2,1)} %bitcast.7, s32[1,512]{1,0:T(1,128)} %bitcast.8, f32[1,512]{1,0:T(1,128)} %bitcast.9, s32[1]{0:T(128)S(6)} %copy.6.live_ref), custom_call_target="tpu_custom_call" | custom-call | tf_op jit(solution)/shard_map/pallas_call | solution.py:191
  58.5 1.9 %broadcast_multiply_fusion = f32[180,720]{1,0:T(8,128)} fusion(f32[180,720]{1,0:T(8,128)} %shard_map.55), kind=kLoop, calls=%fused_computation | loop fusion | flops 129600 | bytes 1036800 | tf_op jit(solution)/shard_map/mul | solution.py:231

commit v3 on v2

--- a/solution.py
+++ b/solution.py
@@ -48,15 +48,21 @@
             device_id=device, device_id_type=MESH,
         )
 
-    load_acts = pltpu.make_async_copy(acts_hbm, acts_raw, load_sems.at[0])
-    load_acts.start()
     grad_order = (1 - half, half)
     load_grads = [
-        pltpu.make_async_copy(grad_hbm.at[g], grad_raw.at[g], load_sems.at[1 + i])
+        pltpu.make_async_copy(grad_hbm.at[g], grad_raw.at[g], load_sems.at[outer + i])
         for i, g in enumerate(grad_order)
     ]
-    for load in load_grads:
-        load.start()
+
+    def load_acts(step):
+        o = target(step)
+        return pltpu.make_async_copy(acts_hbm.at[o], acts_raw.at[o], load_sems.at[step])
+
+    load_grads[0].start()
+    load_acts(0).start()
+    load_grads[1].start()
+    for step in range(1, outer):
+        load_acts(step).start()
 
     barrier = pltpu.get_barrier_semaphore()
     for device in [pair_dev, a_dev, b_dev] + [z_dev(s) for s in range(outer - 1)]:
@@ -67,31 +73,49 @@
     onehot = jnp.where(chosen, 1.0, 0.0).astype(jnp.bfloat16)
     live = lax.broadcasted_iota(jnp.int32, (1, slots), 1) < live_ref[0]
     weight = jnp.where(live, prob_ref[...], 0.0)
-
-    load_acts.wait()
-    rows = acts.shape[2]
-    for k in range(outer * 4):
-        acts[k % 2, k // 2] = acts_raw[k * rows : (k + 1) * rows, :]
-    pl.semaphore_wait(barrier, outer + 2)
-    acts_copy = remote(
-        acts.at[1 - core], peer_acts, (pair_sems.at[0], pair_sems.at[1]), pair_dev
-    )
-    acts_copy.start()
-
-    grad_copies = []
-    for i, g in enumerate(grad_order):
+    rows = acts.shape[3]
+
+    def copy_grad(i):
+        g = grad_order[i]
+        return remote(
+            mine.at[g], peer.at[g],
+            (pair_sems.at[0, outer + i], pair_sems.at[1, outer + i]), pair_dev,
+        )
+
+    def copy_acts(step):
+        o = target(step)
+        return remote(
+            acts.at[1 - core, o], peer_acts.at[o],
+            (pair_sems.at[0, step], pair_sems.at[1, step]), pair_dev,
+        )
+
+    def weigh(i):
+        g = grad_order[i]
         load_grads[i].wait()
         picked = jnp.dot(grad_raw[g], onehot, preferred_element_type=jnp.float32)
         mine[g] = (picked * weight).astype(jnp.bfloat16)
-        copy = remote(
-            mine.at[g], peer.at[g],
-            (pair_sems.at[2 + 2 * i], pair_sems.at[3 + 2 * i]), pair_dev,
-        )
-        copy.start()
-        grad_copies.append(copy)
-    acts_copy.wait_recv()
-    for copy in grad_copies:
-        copy.wait_recv()
+
+    def divide(step):
+        o = target(step)
+        load_acts(step).wait()
+        for k in range(4):
+            acts[k % 2, o, k // 2] = acts_raw[o, k * rows : (k + 1) * rows, :]
+
+    weigh(0)
+    pl.semaphore_wait(barrier, outer + 2)
+    copy_grad(0).start()
+    divide(0)
+    copy_acts(0).start()
+    weigh(1)
+    copy_grad(1).start()
+
+    def feed(step, carry):
+        divide(step)
+        copy_acts(step).start()
+        return carry
+
+    lax.fori_loop(1, outer, feed, 0)
+    copy_grad(0).wait_recv()
 
     def contract(left, right):
         return lax.dot_general(
@@ -99,10 +123,10 @@
         )
 
     def term(step, a, b):
-        row = target(step) * 2 + b * (1 - core) + a * core
+        o, m = target(step), b * (1 - core) + a * core
         column = a * (1 - core) + b * core
-        return contract(acts[core, row], mine[column]) + contract(
-            peer_acts[row], peer[column]
+        return contract(acts[core, o, m], mine[column]) + contract(
+            peer_acts[o, m], peer[column]
         )
 
     def copy_a(step, k):
@@ -123,12 +147,10 @@
             (z_sems.at[0, step], z_sems.at[1, step]), z_dev(step),
         )
 
-    def first(step, carry):
-        for k in range(2):
-            b = 1 - my_b if k == 0 else my_b
-            send_a[step, k] = term(step, 1 - my_a, b).astype(jnp.bfloat16)
-            copy_a(step, k).start()
-        return carry
+    def first(step, k):
+        b = 1 - my_b if k == 0 else my_b
+        send_a[step, k] = term(step, 1 - my_a, b).astype(jnp.bfloat16)
+        copy_a(step, k).start()
 
     def second(step):
         total = term(step, my_a, 1 - my_b)
@@ -142,27 +164,51 @@
         copy_a(step, 1).wait_recv()
         total = total + recv_a[step, 1].astype(jnp.float32)
         copy_b(step).wait_recv()
-        return total + recv_b[step].astype(jnp.float32)
-
-    def later(step, carry):
-        second(step)
-        send_z[step - 1] = third(step - 1).astype(jnp.bfloat16)
-        copy_z(step - 1).start()
-        return carry
-
-    lax.fori_loop(0, outer, first, 0)
-    second(0)
-    lax.fori_loop(1, outer, later, 0)
-    out_ref[...] = third(outer - 1)
+        total = total + recv_b[step].astype(jnp.float32)
+        send_z[step] = total.astype(jnp.bfloat16)
+        copy_z(step).start()
+
+    def stage(step, carry):
+        @pl.when(step < outer)
+        def _():
+            copy_acts(step).wait_recv()
+            first(step, 0)
+
+        @pl.when(step == 1)
+        def _():
+            copy_grad(1).wait_recv()
+
+        @pl.when((step >= 1) & (step <= outer))
+        def _():
+            first(step - 1, 1)
+
+        @pl.when(step >= 2)
+        def _():
+            second(step - 2)
+
+        @pl.when(step >= 3)
+        def _():
+            third(step - 3)
+
+        return carry
+
+    lax.fori_loop(0, outer + 2, stage, 0)
+    last = outer - 1
+    out_ref[...] = term(last, my_a, my_b)
 
     def add(step, carry):
         copy_z(step).wait_recv()
         out_ref[...] += recv_z[step].astype(jnp.float32)
         return carry
 
-    lax.fori_loop(0, outer - 1, add, 0)
+    lax.fori_loop(0, last, add, 0)
+    copy_a(last, 1).wait_recv()
+    out_ref[...] += recv_a[last, 1].astype(jnp.float32)
+    copy_b(last).wait_recv()
+    out_ref[...] += recv_b[last].astype(jnp.float32)
 
     def drain(step, carry):
+        copy_acts(step).wait_send()
         copy_a(step, 0).wait_send()
         copy_a(step, 1).wait_send()
         copy_b(step).wait_send()
@@ -175,9 +221,8 @@
         return carry
 
     lax.fori_loop(0, outer - 1, drain_z, 0)
-    acts_copy.wait_send()
-    for copy in grad_copies:
-        copy.wait_send()
+    copy_grad(0).wait_send()
+    copy_grad(1).wait_send()
 
 
 def shards(expert_act, grad_out, slot_token, slot_prob, live_count):
@@ -200,10 +245,10 @@
         ],
         out_specs=pl.BlockSpec(memory_space=pltpu.VMEM),
         scratch_shapes=[
-            pltpu.VMEM((hidden, slots), bf16),
+            pltpu.VMEM((outer, 4 * rows, slots), bf16),
             pltpu.VMEM((halves, columns, tokens), bf16),
-            pltpu.VMEM((2, outer * 2, rows, slots), bf16),
-            pltpu.VMEM((outer * 2, rows, slots), bf16),
+            pltpu.VMEM((2, outer, 2, rows, slots), bf16),
+            pltpu.VMEM((outer, 2, rows, slots), bf16),
             pltpu.VMEM((halves, columns, slots), bf16),
             pltpu.VMEM((halves, columns, slots), bf16),
             pltpu.VMEM((outer, 2, rows, columns), bf16),
@@ -212,8 +257,8 @@
             pltpu.VMEM((outer, rows, columns), bf16),
             pltpu.VMEM((outer - 1, rows, columns), bf16),
             pltpu.VMEM((outer - 1, rows, columns), bf16),
-            dma((3,)),
-            dma((6,)),
+            dma((outer + 2,)),
+            dma((2, outer + 2)),
             dma((2, outer, 2)),
             dma((2, outer)),
             dma((2, outer - 1)),
@@ -222,7 +267,7 @@
             collective_id=0, has_side_effects=True, vmem_limit_bytes=60 * 2**20
         ),
     )(
-        expert_act.T,
+        expert_act.T.reshape(outer, 4 * rows, slots),
         grad_out.T.reshape(halves, columns, tokens),
         slot_token[None, :],
         slot_prob[None, :],

time: 60.6 us -> 57.4 us (0.947)
  Pallas kernels: 57.9 us -> 54.6 us
    pallas_call x1, Pallas kernels: 57.9 us -> 54.6 us  [shards(): pl.pallas_call(functools.partial(kernel, outer), out_shape=jax.ShapeDtype...]
where the time goes in v3:
time: 57.4 us; the launch traced here: 57.2 us
  Pallas kernels  54.6 us (95%)
  other arithmetic  1.9 us (3%)
  between operations  0.66 us (1%)
    pallas_call x1, Pallas kernels, shards(): pl.pallas_call(functools.partial(kernel, outer), out_shape=jax.ShapeDtype...  54.6 us
    mul x1, other arithmetic, shards(): return total * scaling  1.9 us

profile of v3, /device:TPU:0, one launch (start us, length us, event | category | flops | bytes accessed | tf_op | source)
XLA Modules:
  0.0 57.2 jit_solution(12562941704669246190)
XLA Ops:
  0.7 54.6 %shard_map.55 = f32[180,720]{1,0:T(8,128)} custom-call(bf16[4,720,512]{2,1,0:T(8,128)(2,1)} %bitcast.8, bf16[2,720,1024]{2,1,0:T(8,128)(2,1)} %bitcast.9, s32[1,512]{1,0:T(1,128)} %bitcast.10, f32[1,512]{1,0:T(1,128)} %bitcast.11, s32[1]{0:T(128)S(6)} %copy.6.live_ref), custom_call_target="tpu_custom_call" | custom-call | tf_op jit(solution)/shard_map/pallas_call | solution.py:236
  55.3 1.9 %broadcast_multiply_fusion = f32[180,720]{1,0:T(8,128)} fusion(f32[180,720]{1,0:T(8,128)} %shard_map.55), kind=kLoop, calls=%fused_computation | loop fusion | flops 129600 | bytes 1036800 | tf_op jit(solution)/shard_map/mul | solution.py:276

commit v4 on v3

--- a/solution.py
+++ b/solution.py
@@ -40,7 +40,8 @@
         return {"dp": dp + (target(step) - own) * 4, "tensor": half}
 
     def target(step):
-        return lax.rem(own + 1 + step, outer)
+        offset = outer // 2 + step // 2 - (step % 2) * step
+        return lax.rem(own + offset, outer)
 
     def remote(src, dst, sems, device):
         return pltpu.make_async_remote_copy(
@@ -60,9 +61,6 @@
 
     load_grads[0].start()
     load_acts(0).start()
-    load_grads[1].start()
-    for step in range(1, outer):
-        load_acts(step).start()
 
     barrier = pltpu.get_barrier_semaphore()
     for device in [pair_dev, a_dev, b_dev] + [z_dev(s) for s in range(outer - 1)]:
@@ -91,7 +89,6 @@
 
     def weigh(i):
         g = grad_order[i]
-        load_grads[i].wait()
         picked = jnp.dot(grad_raw[g], onehot, preferred_element_type=jnp.float32)
         mine[g] = (picked * weight).astype(jnp.bfloat16)
 
@@ -101,11 +98,16 @@
         for k in range(4):
             acts[k % 2, o, k // 2] = acts_raw[o, k * rows : (k + 1) * rows, :]
 
+    load_grads[0].wait()
+    load_grads[1].start()
     weigh(0)
+    for step in range(1, outer):
+        load_acts(step).start()
     pl.semaphore_wait(barrier, outer + 2)
     copy_grad(0).start()
     divide(0)
     copy_acts(0).start()
+    load_grads[1].wait()
     weigh(1)
     copy_grad(1).start()
 

time: 57.4 us -> 54.3 us (0.946)
  Pallas kernels: 54.6 us -> 51.5 us
    pallas_call x1, Pallas kernels: 54.6 us -> 51.5 us  [shards(): pl.pallas_call(functools.partial(kernel, outer), out_shape=jax.ShapeDtype...]
where the time goes in v4:
time: 54.3 us; the launch traced here: 54.1 us
  Pallas kernels  51.5 us (95%)
  other arithmetic  1.9 us (3%)
  between operations  0.66 us (1%)
    pallas_call x1, Pallas kernels, shards(): pl.pallas_call(functools.partial(kernel, outer), out_shape=jax.ShapeDtype...  51.5 us
    mul x1, other arithmetic, shards(): return total * scaling  1.9 us

profile of v4, /device:TPU:0, one launch (start us, length us, event | category | flops | bytes accessed | tf_op | source)
XLA Modules:
  0.0 54.1 jit_solution(17055147859721305739)
XLA Ops:
  0.7 51.5 %shard_map.55 = f32[180,720]{1,0:T(8,128)} custom-call(bf16[4,720,512]{2,1,0:T(8,128)(2,1)} %bitcast.8, bf16[2,720,1024]{2,1,0:T(8,128)(2,1)} %bitcast.9, s32[1,512]{1,0:T(1,128)} %bitcast.10, f32[1,512]{1,0:T(1,128)} %bitcast.11, s32[1]{0:T(128)S(6)} %copy.6.live_ref), custom_call_target="tpu_custom_call" | custom-call | tf_op jit(solution)/shard_map/pallas_call | solution.py:238
  52.2 1.9 %broadcast_multiply_fusion = f32[180,720]{1,0:T(8,128)} fusion(f32[180,720]{1,0:T(8,128)} %shard_map.55), kind=kLoop, calls=%fused_computation | loop fusion | flops 129600 | bytes 1036800 | tf_op jit(solution)/shard_map/mul | solution.py:278

commit v5 on v4

--- a/solution.py
+++ b/solution.py
@@ -266,7 +266,7 @@
             dma((2, outer - 1)),
         ],
         compiler_params=pltpu.CompilerParams(
-            collective_id=0, has_side_effects=True, vmem_limit_bytes=60 * 2**20
+            collective_id=0, has_side_effects=True, vmem_limit_bytes=53 * 2**20
         ),
     )(
         expert_act.T.reshape(outer, 4 * rows, slots),

time: 54.3 us -> 53.2 us (0.980)
  Pallas kernels: 51.5 us -> 50.1 us
  local copies, waits for them, and re-layouts: 0 us -> 1.36 us
  other arithmetic: 1.9 us -> 0.85 us
    pallas_call x1, Pallas kernels: 51.5 us -> 50.1 us  [shards(): pl.pallas_call(functools.partial(kernel, outer), out_shape=jax.ShapeDtype...]
    unnamed x0 -> x4, local copies, waits for them, and re-layouts: none -> 1.36 us
    mul x1, other arithmetic: 1.9 us -> 0.85 us  [shards(): return total * scaling]
where the time goes in v5:
time: 53.2 us; the launch traced here: 53 us
  Pallas kernels  50.1 us (94%)
  local copies, waits for them, and re-layouts  1.36 us (3%)
  other arithmetic  0.85 us (2%)
  between operations  0.67 us (1%)
    pallas_call x1, Pallas kernels, shards(): pl.pallas_call(functools.partial(kernel, outer), out_shape=jax.ShapeDtype...  50.1 us
    unnamed x4, local copies, waits for them, and re-layouts  1.36 us

profile of v5, /device:TPU:0, one launch (start us, length us, event | category | flops | bytes accessed | tf_op | source)
XLA Modules:
  0.0 53.0 jit_solution(2812924463170082394)
XLA Ops:
  0.7 0.0 copy-start
  0.7 0.7 %copy-done = s32[512]{0:T(512)S(1)} copy-done((s32[512]{0:T(512)S(1)}, s32[512]{0:T(512)}, u32[]{:S(2)}) %copy-start) | copy-done | bytes 2072
  1.3 0.0 copy-start.1
  1.3 0.7 %copy-done.1 = f32[512]{0:T(512)S(1)} copy-done((f32[512]{0:T(512)S(1)}, f32[512]{0:T(512)}, u32[]{:S(2)}) %copy-start.1) | copy-done | bytes 2072
  2.0 50.1 %shard_map.55 = f32[180,720]{1,0:T(8,128)S(1)} custom-call(bf16[4,720,512]{2,1,0:T(8,128)(2,1)} %bitcast.10, bf16[2,720,1024]{2,1,0:T(8,128)(2,1)} %bitcast.11, s32[1,512]{1,0:T(1,128)S(1)} %bitcast.8, f32[1,512]{1,0:T(1,128)S(1)} %bitcast.9, s32[1]{0:T(128)S(6)} %copy.6.live_ref), custom_call_target="tpu_custom_call" | custom-call | tf_op jit(solution)/shard_map/pallas_call | solution.py:238
  52.1 0.8 %broadcast_multiply_fusion = f32[180,720]{1,0:T(8,128)} fusion(f32[180,720]{1,0:T(8,128)S(1)} %shard_map.55), kind=kLoop, calls=%fused_computation | loop fusion | flops 129600 | bytes 1036800 | tf_op jit(solution)/shard_map/mul | solution.py:278
Async XLA Ops:
  0.7 0.7 %copy-start = (s32[512]{0:T(512)S(1)}, s32[512]{0:T(512)}, u32[]{:S(2)}) copy-start(s32[512]{0:T(512)} %param.7) | copy-start | bytes 6148
  1.3 0.7 %copy-start.1 = (f32[512]{0:T(512)S(1)}, f32[512]{0:T(512)}, u32[]{:S(2)}) copy-start(f32[512]{0:T(512)} %param.8) | copy-start | bytes 6148
